TPU v7x, 32 devices: a whole 2x2x4 slice. The times are simulated.
32 devices in a mesh: dom: 32 (over z, y, x, core).
Axes of the slice: x: 2, y: 2, z: 4, core: 2. Of those that a mesh axis runs over, the one named last changes fastest.
Arguments:
- features: bfloat16 [32768, 512], P('dom'), may hold values from -6 to 6
- embeddings: bfloat16 [32768, 128], P('dom'), may hold values from -6 to 6
- tile_values: bfloat16 [256, 4, 128, 128], P('dom'), may hold values from -4 to 4
- tile_columns: int32 [256, 4], P('dom'), may hold values from 0 to 11
- send_blocks: int32 [32, 2, 2], P('dom'), may hold values from 0 to 7
- send_count: int32 [32, 2], P('dom'), may hold values from 1 to 2, as said below
- hub_rows: int32 [64], P('dom'), may hold values from 0 to 1023, as said below
- hub_weight: bfloat16 [32768, 64], P('dom'), may hold values from -4 to 4
- degree: int32 [32768], P('dom'), may hold values from 16 to 64
Outputs:
- hop_features: bfloat16 [3, 32768, 512], P(None, 'dom')
- hop_embeddings: bfloat16 [3, 32768, 128], P(None, 'dom')
Inputs may be any that keep to these rules, and one draw needn't show every extreme that they name: `send_count`: some partition sends 2 blocks to its right and some to its left. `hub_rows`: the 2 hub rows of each partition are distinct local row numbers.
All inputs are finite; a program needn't handle non-finite values.
Results may differ from a plain program's by a relative error of at most 0.012.
Values may be sent and summed in bfloat16 or wider, within the bound.
A program may use at most 64 MiB of HBM per device.

v0:
```python
import jax
import jax.numpy as jnp
from jax import lax
from jax.sharding import PartitionSpec as P

HOPS = 3


def shifted(value, axis, steps):
    count = lax.axis_size(axis)
    initial, last = (max(0, -steps), min(count, count - steps))
    return lax.ppermute(value, axis, [(source, source + steps) for source in range(initial, last)])


def body(
    features,
    embeddings,
    tile_values,
    tile_columns,
    send_blocks,
    send_count,
    hub_rows,
    hub_weight,
    degree,
):
    row_count = features.shape[0]
    tile_size = tile_values.shape[2]
    block_count = row_count // tile_size
    send_most = send_blocks.shape[2]
    feature_width = features.shape[1] + embeddings.shape[1]
    rim_rows = send_most * tile_size
    inverse_root = lax.rsqrt(degree.astype(jnp.float32))[:, None]
    current = jnp.concatenate([features, embeddings], axis=1)
    listed = send_blocks[0].reshape(-1)
    live_slots = (jnp.arange(send_most, dtype=jnp.int32)[None, :] < send_count[0][:, None]).reshape(
        -1
    )
    results = []
    for hop_index in range(HOPS):
        scaled = (current.astype(jnp.float32) * inverse_root).astype(jnp.bfloat16)
        blocked = scaled.reshape(block_count, tile_size, feature_width)
        outgoing = blocked[listed]
        outgoing = jnp.where(live_slots[:, None, None], outgoing, jnp.zeros_like(outgoing))
        outgoing = outgoing.reshape(2 * rim_rows, feature_width)
        hub_local = scaled[hub_rows]
        gathered_hubs = lax.all_gather(hub_local, "dom", axis=0, tiled=True)
        hub_sum = jnp.dot(hub_weight, gathered_hubs, preferred_element_type=jnp.float32)
        from_left = shifted(outgoing[rim_rows:], "dom", 1)
        from_right = shifted(outgoing[:rim_rows], "dom", -1)
        extended = jnp.concatenate(
            [
                blocked,
                from_left.reshape(send_most, tile_size, feature_width),
                from_right.reshape(send_most, tile_size, feature_width),
            ],
            axis=0,
        )
        picked = extended[tile_columns]
        local_part = jnp.einsum(
            "bkij,bkjw->biw", tile_values, picked, preferred_element_type=jnp.float32
        )
        summed = local_part.reshape(row_count, feature_width) + hub_sum
        current = (summed * inverse_root).astype(jnp.bfloat16)
        results.append(current)
    stacked = jnp.stack(results)
    split_at = features.shape[1]
    return (stacked[:, :, :split_at], stacked[:, :, split_at:])


def solution(mesh):
    placed = (
        P("dom", None),
        P("dom", None),
        P("dom", None, None, None),
        P("dom", None),
        P("dom", None, None),
        P("dom", None),
        P("dom"),
        P("dom", None),
        P("dom"),
    )
    return jax.shard_map(
        body,
        mesh=mesh,
        in_specs=placed,
        out_specs=(P(None, "dom", None), P(None, "dom", None)),
        check_vma=False,
    )
```

profile of v0, /device:TPU:1, one launch (start us, length us, event | category | flops | bytes accessed | tf_op | source)
XLA Modules:
  0.0 218.9 jit_solution(10857633315471224269)
XLA Ops:
  0.6 0.8 reshape_squeeze.3
  1.5 0.7 iota_compare_fusion
  2.3 0.7 convert_rsqrt_fusion
  3.0 1.6 multiply_convert_fusion.3
  4.7 1.5 gather_fusion
  6.1 1.2 broadcast_select_fusion.2
  7.4 0.9 fusion.11
  8.3 1.9 collective-permute-start.1
  10.2 4.5 %collective-permute-start = (bf16[256,640]{1,0:T(8,128)(2,1)}, bf16[256,640]{1,0:T(8,128)(2,1)}, u32[]{:S(2)}, u32[]{:S(2)}) collective-permute-start(bf16[256,640]{1,0:T(8,128)(2,1)} %bitcast.5), channel_id=1, source_target_pairs={{0,1},{1,2},{2,3},{3,4},{4,5},{5,6},{6,7},{7,8},{8,9},{9,10},{10,1... | collective-permute-start | bytes 983048 | tf_op jit(solution)/shard_map/ppermute | solution.py:12
  14.7 1.8 copy.43
  16.5 1.3 copy.42
  17.8 1.6 multiply_convert_fusion.2
  19.6 1.5 copy.44
  21.1 2.0 gather_fusion.2
  23.2 42.1 %all-gather.3 = bf16[32,2,640]{2,1,0:T(2,128)(2,1)S(1)} all-gather(bf16[1,2,640]{2,1,0:T(2,128)(2,1)S(1)} %bitcast.103), channel_id=2, replica_groups=mesh['dom'=32] {'dom'}, dimensions={0}, use_global_device_ids=true | all-gather | bytes 84480 | tf_op jit(solution)/shard_map/all_gather | solution.py:46
  65.3 1.8 pad_maximum_fusion.1
  67.1 3.5 %gather_fusion.1 = bf16[32,128,640]{2,1,0:T(8,128)(2,1)} fusion(bf16[12,128,640]{2,1,0:T(8,128)(2,1)S(1)} %pad_maximum_fusion.1, s32[1024]{0:T(1024)S(1)} %pad_clamp_fusion.1), kind=kCustom, calls=%fused_computation.1 | custom fusion | bytes 10485888 | tf_op jit(solution)/shard_map/gather | solution.py:58
  70.6 5.0 %fusion.12 = f32[8,640,128,1]{1,2,3,0:T(8,128)} fusion(bf16[8,4,128,128]{3,2,1,0:T(8,128)(2,1)S(1)} %copy-done, bf16[8,4,128,640]{3,2,1,0:T(8,128)(2,1)} %bitcast.82), kind=kOutput, calls=%fused_computation.44 | convolution fusion | flops 671088640 | bytes 8912896 | tf_op jit(solution)/shard_map/bkij,bkjw->biw/dot_general | solution.py:59
  75.6 3.3 %copy.45 = f32[1024,640]{0,1:T(8,128)} copy(f32[1024,640]{1,0:T(8,128)} %bitcast.88) | data formatting | bytes 5242880 | tf_op jit(solution)/shard_map/reshape | solution.py:62
  78.9 3.8 %multiply_convert_fusion.1 = (bf16[1024,640]{0,1:T(8,128)(2,1)}, bf16[1024,640]{0,1:T(8,128)(2,1)}) fusion(f32[1024]{0:T(1024)S(1)} %get-tuple-element.14, f32[1024,640]{0,1:T(8,128)} %copy.45, bf16[64,640]{1,0:T(8,128)(2,1)S(1)} %reshape.194, bf16[1024,64]{0,1:T(8,128)(2,1)S(1)} %copy-done.7), kind=kOutput, calls=%fused_computation.20 | convolution fusion | flops 87818240 | bytes 5459968 | tf_op jit(solution)/shard_map/dot_general | solution.py:47
  82.7 1.7 copy.61
  84.4 0.7 gather_fusion.3
  85.3 2.1 collective-permute-start.3
  87.4 3.5 %collective-permute-start.2 = (bf16[256,640]{1,0:T(8,128)(2,1)S(1)}, bf16[256,640]{1,0:T(8,128)(2,1)}, u32[]{:S(2)}, u32[]{:S(2)}) collective-permute-start(bf16[256,640]{1,0:T(8,128)(2,1)S(1)} %bitcast.98), channel_id=1, source_target_pairs={{0,1},{1,2},{2,3},{3,4},{4,5},{5,6},{6,7},{7,8},{8,9},{9,10},{10,1... | collective-permute-start | bytes 983048 | tf_op jit(solution)/shard_map/ppermute | solution.py:12
  90.9 1.3 gather_fusion.5
  92.1 37.1 %all-gather.4 = bf16[32,2,640]{2,1,0:T(2,128)(2,1)S(1)} all-gather(bf16[1,2,640]{2,1,0:T(2,128)(2,1)} %bitcast.105), channel_id=3, replica_groups=mesh['dom'=32] {'dom'}, dimensions={0}, use_global_device_ids=true | all-gather | bytes 84480 | tf_op jit(solution)/shard_map/all_gather | solution.py:46
  129.2 0.7 reshape.196
  129.9 1.7 pad_maximum_fusion.2
  131.6 3.5 %gather_fusion.4 = bf16[32,128,640]{2,1,0:T(8,128)(2,1)} fusion(bf16[12,128,640]{2,1,0:T(8,128)(2,1)S(1)} %pad_maximum_fusion.2, s32[1024]{0:T(1024)S(1)} %copy-done.14), kind=kCustom, calls=%fused_computation.4 | custom fusion | bytes 10485888 | tf_op jit(solution)/shard_map/gather | solution.py:58
  135.1 5.0 %fusion.13 = f32[8,640,128,1]{1,2,3,0:T(8,128)} fusion(bf16[8,4,128,128]{3,2,1,0:T(8,128)(2,1)S(1)} %copy-done, bf16[8,4,128,640]{3,2,1,0:T(8,128)(2,1)} %bitcast.83), kind=kOutput, calls=%fused_computation.45 | convolution fusion | flops 671088640 | bytes 8912896 | tf_op jit(solution)/shard_map/bkij,bkjw->biw/dot_general | solution.py:59
  140.1 3.3 %copy.59 = f32[1024,640]{0,1:T(8,128)} copy(f32[1024,640]{1,0:T(8,128)} %bitcast.89) | data formatting | bytes 5242880 | tf_op jit(solution)/shard_map/reshape | solution.py:62
  143.4 3.8 %multiply_convert_fusion = (bf16[1024,640]{0,1:T(8,128)(2,1)}, bf16[1024,640]{0,1:T(8,128)(2,1)}) fusion(f32[1024]{0:T(1024)S(1)} %copy-done.11, f32[1024,640]{0,1:T(8,128)} %copy.59, bf16[64,640]{1,0:T(8,128)(2,1)S(1)} %copy-done.8, bf16[1024,64]{0,1:T(8,128)(2,1)S(1)} %copy-done.7), kind=kOutput, calls=%fused_computation.19 | convolution fusion | flops 87818240 | bytes 5459968 | tf_op jit(solution)/shard_map/dot_general | solution.py:47
  147.2 1.7 copy.62
  148.9 0.8 gather_fusion.6
  149.9 2.1 collective-permute-start.5
  152.0 3.5 %collective-permute-start.4 = (bf16[256,640]{1,0:T(8,128)(2,1)S(1)}, bf16[256,640]{1,0:T(8,128)(2,1)}, u32[]{:S(2)}, u32[]{:S(2)}) collective-permute-start(bf16[256,640]{1,0:T(8,128)(2,1)S(1)} %bitcast.97), channel_id=1, source_target_pairs={{0,1},{1,2},{2,3},{3,4},{4,5},{5,6},{6,7},{7,8},{8,9},{9,10},{10,1... | collective-permute-start | bytes 983048 | tf_op jit(solution)/shard_map/ppermute | solution.py:12
  155.5 1.3 gather_fusion.8
  156.7 37.3 %all-gather.5 = bf16[32,2,640]{2,1,0:T(2,128)(2,1)S(1)} all-gather(bf16[1,2,640]{2,1,0:T(2,128)(2,1)} %bitcast.104), channel_id=4, replica_groups=mesh['dom'=32] {'dom'}, dimensions={0}, use_global_device_ids=true | all-gather | bytes 84480 | tf_op jit(solution)/shard_map/all_gather | solution.py:46
  194.0 0.7 reshape.198
  194.7 1.7 pad_maximum_fusion.3
  196.4 3.5 %gather_fusion.7 = bf16[32,128,640]{2,1,0:T(8,128)(2,1)} fusion(bf16[12,128,640]{2,1,0:T(8,128)(2,1)S(1)} %pad_maximum_fusion.3, s32[1024]{0:T(1024)S(1)} %copy-done.15), kind=kCustom, calls=%fused_computation.7 | custom fusion | bytes 10485888 | tf_op jit(solution)/shard_map/gather | solution.py:58
  199.9 5.0 %fusion.14 = f32[8,640,128,1]{1,2,3,0:T(8,128)} fusion(bf16[8,4,128,128]{3,2,1,0:T(8,128)(2,1)S(1)} %copy-done, bf16[8,4,128,640]{3,2,1,0:T(8,128)(2,1)} %bitcast.81), kind=kOutput, calls=%fused_computation.46 | convolution fusion | flops 671088640 | bytes 8912896 | tf_op jit(solution)/shard_map/bkij,bkjw->biw/dot_general | solution.py:59
  204.9 3.3 %copy.60 = f32[1024,640]{0,1:T(8,128)} copy(f32[1024,640]{1,0:T(8,128)} %bitcast.90) | data formatting | bytes 5242880 | tf_op jit(solution)/shard_map/reshape | solution.py:62
  208.2 2.4 %fusion.6 = bf16[1,1024,640]{1,2,0:T(8,128)(2,1)S(1)} fusion(f32[1024,640]{0,1:T(8,128)} %copy.60, bf16[64,640]{1,0:T(8,128)(2,1)S(1)} %copy-done.9, bf16[1024,64]{0,1:T(8,128)(2,1)S(1)} %copy-done.7, f32[1024]{0:T(1024)S(1)} %copy-done.12), kind=kOutput, calls=%fused_computation.26 | convolution fusion | flops 85852160 | bytes 4149248 | tf_op jit(solution)/shard_map/dot_general | solution.py:47
  210.7 0.5 pad_maximum_fusion
  211.2 1.9 slice.80
  213.1 4.6 %copy.54 = bf16[3,1024,512]{2,1,0:T(8,128)(2,1)} copy(bf16[3,1024,512]{1,2,0:T(8,128)(2,1)} %slice.80) | data formatting | bytes 6291456
  217.8 1.2 copy.55
  (65 shorter events, 0.9 us)
Async XLA Ops:
  0.6 70.0 %copy-start = (bf16[8,4,128,128]{3,2,1,0:T(8,128)(2,1)S(1)}, bf16[8,4,128,128]{3,2,1,0:T(8,128)(2,1)}, u32[]{:S(2)}) copy-start(bf16[8,4,128,128]{3,2,1,0:T(8,128)(2,1)} %param.11) | copy-start | bytes 3145732
  2.3 82.8 %copy-start.18 = (pred[4]{0:T(512)(128)(4,1)}, pred[4]{0:T(512)(128)(4,1)S(1)}, u32[]{:S(2)}) copy-start(pred[4]{0:T(512)(128)(4,1)S(1)} %lt.48) | copy-start | bytes 16
  2.3 82.1 %copy-start.16 = (s32[1024]{0:T(1024)}, s32[1024]{0:T(1024)S(1)}, u32[]{:S(2)}) copy-start(s32[1024]{0:T(1024)S(1)} %pad_clamp_fusion.2) | copy-start | bytes 12292
  3.0 75.9 %copy-start.10 = (f32[1024]{0:T(1024)}, f32[1024]{0:T(1024)S(1)}, u32[]{:S(2)}) copy-start(f32[1024]{0:T(1024)S(1)} %get-tuple-element.14) | copy-start | bytes 12292
  4.6 13.2 %copy-start.5 = (bf16[8,128,640]{2,1,0:T(8,128)(2,1)}, bf16[8,128,640]{2,1,0:T(8,128)(2,1)S(1)}, u32[]{:S(2)}) copy-start(bf16[8,128,640]{2,1,0:T(8,128)(2,1)S(1)} %multiply_convert_fusion.3) | copy-start | bytes 3932164
  4.7 11.8 %copy-start.6 = (bf16[1024,512]{1,0:T(8,128)(2,1)S(1)}, bf16[1024,512]{1,0:T(8,128)(2,1)}, u32[]{:S(2)}) copy-start(bf16[1024,512]{1,0:T(8,128)(2,1)} %param.9) | copy-start | bytes 3145732
  6.1 11.7 %copy-start.20 = (s32[8,4]{0,1:T(4,128)S(1)}, s32[8,4]{0,1:T(4,128)}, u32[]{:S(2)}) copy-start(s32[8,4]{0,1:T(4,128)} %param.12) | copy-start | bytes 388
  8.3 57.1 %collective-permute-start.1 = (bf16[256,640]{1,0:T(8,128)(2,1)}, bf16[256,640]{1,0:T(8,128)(2,1)}, u32[]{:S(2)}, u32[]{:S(2)}) collective-permute-start(bf16[256,640]{1,0:T(8,128)(2,1)} %bitcast.7), channel_id=1, source_target_pairs={{1,0},{2,1},{3,2},{4,3},{5,4},{6,5},{7,6},{8,7},{9,8},{10,9},{11,1... | collective-permute-start | bytes 983048 | tf_op jit(solution)/shard_map/ppermute | solution.py:12
  10.2 9.3 %copy-start.21 = (s32[2]{0:T(128)S(1)}, s32[2]{0:T(128)}, u32[]{:S(2)}) copy-start(s32[2]{0:T(128)} %param.15) | copy-start | bytes 28
  10.2 55.1 %collective-permute-start = (bf16[256,640]{1,0:T(8,128)(2,1)}, bf16[256,640]{1,0:T(8,128)(2,1)}, u32[]{:S(2)}, u32[]{:S(2)}) collective-permute-start(bf16[256,640]{1,0:T(8,128)(2,1)} %bitcast.5), channel_id=1, source_target_pairs={{0,1},{1,2},{2,3},{3,4},{4,5},{5,6},{6,7},{7,8},{8,9},{9,10},{10,1... | collective-permute-start | bytes 983048 | tf_op jit(solution)/shard_map/ppermute | solution.py:12
  21.1 2.1 copy-start.17
  65.3 5.3 %copy-start.13 = (s32[1024]{0:T(1024)}, s32[1024]{0:T(1024)S(1)}, u32[]{:S(2)}) copy-start(s32[1024]{0:T(1024)S(1)} %pad_clamp_fusion.1) | copy-start | bytes 12292
  75.6 3.3 %copy-start.7 = (bf16[1024,64]{0,1:T(8,128)(2,1)S(1)}, bf16[1024,64]{0,1:T(8,128)(2,1)}, u32[]{:S(2)}) copy-start(bf16[1024,64]{0,1:T(8,128)(2,1)} %param.16) | copy-start | bytes 393220
  84.4 45.5 %copy-start.4 = (bf16[1024,640]{1,0:T(8,128)(2,1)}, bf16[1024,640]{1,0:T(8,128)(2,1)S(1)}, u32[]{:S(2)}) copy-start(bf16[1024,640]{1,0:T(8,128)(2,1)S(1)} %copy.61) | copy-start | bytes 3932164
  85.3 44.6 %collective-permute-start.3 = (bf16[256,640]{1,0:T(8,128)(2,1)S(1)}, bf16[256,640]{1,0:T(8,128)(2,1)S(1)}, u32[]{:S(2)}, u32[]{:S(2)}) collective-permute-start(bf16[256,640]{1,0:T(8,128)(2,1)S(1)} %bitcast.100), channel_id=1, source_target_pairs={{1,0},{2,1},{3,2},{4,3},{5,4},{6,5},{7,6},{8,7},{9,8},{10,9},{11,1... | collective-permute-start | bytes 983048 | tf_op jit(solution)/shard_map/ppermute | solution.py:12
  87.4 42.5 %collective-permute-start.2 = (bf16[256,640]{1,0:T(8,128)(2,1)S(1)}, bf16[256,640]{1,0:T(8,128)(2,1)}, u32[]{:S(2)}, u32[]{:S(2)}) collective-permute-start(bf16[256,640]{1,0:T(8,128)(2,1)S(1)} %bitcast.98), channel_id=1, source_target_pairs={{0,1},{1,2},{2,3},{3,4},{4,5},{5,6},{6,7},{7,8},{8,9},{9,10},{10,1... | collective-permute-start | bytes 983048 | tf_op jit(solution)/shard_map/ppermute | solution.py:12
  129.9 1.7 copy-start.14
  140.1 3.3 %copy-start.8 = (bf16[64,640]{1,0:T(8,128)(2,1)S(1)}, bf16[64,640]{1,0:T(8,128)(2,1)}, u32[]{:S(2)}) copy-start(bf16[64,640]{1,0:T(8,128)(2,1)} %reshape.196) | copy-start | bytes 245764
  140.1 3.3 %copy-start.11 = (f32[1024]{0:T(1024)S(1)}, f32[1024]{0:T(1024)}, u32[]{:S(2)}) copy-start(f32[1024]{0:T(1024)} %copy-done.10) | copy-start | bytes 12292
  147.2 2.5 %copy-start.19 = (pred[4]{0:T(512)(128)(4,1)S(1)}, pred[4]{0:T(512)(128)(4,1)}, u32[]{:S(2)}) copy-start(pred[4]{0:T(512)(128)(4,1)} %copy-done.18) | copy-start | bytes 16
  148.9 45.8 %copy-start.3 = (bf16[1024,640]{1,0:T(8,128)(2,1)}, bf16[1024,640]{1,0:T(8,128)(2,1)S(1)}, u32[]{:S(2)}) copy-start(bf16[1024,640]{1,0:T(8,128)(2,1)S(1)} %copy.62) | copy-start | bytes 3932164
  149.9 44.8 %collective-permute-start.5 = (bf16[256,640]{1,0:T(8,128)(2,1)S(1)}, bf16[256,640]{1,0:T(8,128)(2,1)S(1)}, u32[]{:S(2)}, u32[]{:S(2)}) collective-permute-start(bf16[256,640]{1,0:T(8,128)(2,1)S(1)} %bitcast.99), channel_id=1, source_target_pairs={{1,0},{2,1},{3,2},{4,3},{5,4},{6,5},{7,6},{8,7},{9,8},{10,9},{11,1... | collective-permute-start | bytes 983048 | tf_op jit(solution)/shard_map/ppermute | solution.py:12
  152.0 42.7 %collective-permute-start.4 = (bf16[256,640]{1,0:T(8,128)(2,1)S(1)}, bf16[256,640]{1,0:T(8,128)(2,1)}, u32[]{:S(2)}, u32[]{:S(2)}) collective-permute-start(bf16[256,640]{1,0:T(8,128)(2,1)S(1)} %bitcast.97), channel_id=1, source_target_pairs={{0,1},{1,2},{2,3},{3,4},{4,5},{5,6},{6,7},{7,8},{8,9},{9,10},{10,1... | collective-permute-start | bytes 983048 | tf_op jit(solution)/shard_map/ppermute | solution.py:12
  194.7 1.7 copy-start.15
  204.9 3.3 %copy-start.9 = (bf16[64,640]{1,0:T(8,128)(2,1)S(1)}, bf16[64,640]{1,0:T(8,128)(2,1)}, u32[]{:S(2)}) copy-start(bf16[64,640]{1,0:T(8,128)(2,1)} %reshape.198) | copy-start | bytes 245764
  204.9 3.3 %copy-start.12 = (f32[1024]{0:T(1024)S(1)}, f32[1024]{0:T(1024)}, u32[]{:S(2)}) copy-start(f32[1024]{0:T(1024)} %copy-done.10) | copy-start | bytes 12292
  208.2 2.4 %copy-start.1 = (bf16[1024,640]{0,1:T(8,128)(2,1)S(1)}, bf16[1024,640]{0,1:T(8,128)(2,1)}, u32[]{:S(2)}) copy-start(bf16[1024,640]{0,1:T(8,128)(2,1)} %get-tuple-element.17) | copy-start | bytes 3932164
  208.2 2.5 %copy-start.2 = (bf16[1024,640]{0,1:T(8,128)(2,1)S(1)}, bf16[1024,640]{0,1:T(8,128)(2,1)}, u32[]{:S(2)}) copy-start(bf16[1024,640]{0,1:T(8,128)(2,1)} %get-tuple-element.19) | copy-start | bytes 3932164
where the time goes:
time: 220 us; the launch traced here: 219 us
  blocking collectives  116 us (53%)
  local copies, waits for them, and re-layouts  47.2 us (21%)
  matrix products  24.9 us (11%)
  starting transfers between devices  17.5 us (8%)
  other arithmetic  11.9 us (5%)
    all_gather x3, blocking collectives, body(): gathered_hubs = lax.all_gather(hub_local, 'dom', axis=0, tiled=True)  116 us
    ppermute x6, starting transfers between devices, shifted(): lax.ppermute(value, axis, [(source, source + steps) for source in range(i...  17.5 us
    dot_general x3, matrix products, body(): jnp.einsum('bkij,bkjw->biw', tile_values, picked, preferred_element_type=...  14.9 us
    gather x3, local copies, waits for them, and re-layouts, body(): picked = extended[tile_columns]  10.5 us
    unnamed x51, local copies, waits for them, and re-layouts  10.4 us
    dot_general x3, matrix products, body(): jnp.dot(hub_weight, gathered_hubs, preferred_element_type=jnp.float32)  9.96 us
    reshape x3, local copies, waits for them, and re-layouts, body(): summed = local_part.reshape(row_count, feature_width) + hub_sum  9.84 us
    concatenate x3, other arithmetic, body(): jnp.concatenate([blocked, from_left.reshape(send_most, tile_size, feature...  5.18 us
  transfers between devices with their start and end apart: 6, of which 0 were waited for; matrix products, arithmetic and copies ran while one was open for 6% of the time, Pallas kernels for 0%

commit v1 on v0

v1 whole, which is shorter than its diff:
```python
import functools

import jax
import jax.numpy as jnp
from jax import lax
from jax.experimental import pallas as pl
from jax.experimental.pallas import tpu as pltpu
from jax.sharding import PartitionSpec as P

HOPS = 3
LANES = 128
MESH = pl.DeviceIdType.MESH


def kernel(
    n, sizes, cols_ref, listed_ref, count_ref, hubs_ref,
    features, embeddings, tiles, weight, degree,
    out_f, out_e, *scratch,
):
    blocks, tile, taps, send_most, hub_dev, chunks, f_chunks = sizes
    per = tile // 16
    pairs = HOPS * chunks
    scratch = list(scratch)
    take = lambda count: [scratch.pop(0) for _ in range(count)]
    locals_, groups, exts, sends, hub_sends, hub_bufs = (take(pairs) for _ in range(6))
    inv, rim_send_sem, rim_recv_sem, hub_send_sem, hub_recv_sem = scratch
    me = lax.axis_index("dom")

    barrier = pltpu.get_barrier_semaphore()

    def greet(step, carry):
        pl.semaphore_signal(
            barrier, inc=1, device_id=(lax.rem(me + step, n),), device_id_type=MESH
        )
        return carry

    lax.fori_loop(1, n, greet, 0)

    roots = lax.rsqrt(degree[...].astype(jnp.float32)).T
    for b in range(blocks):
        inv[b] = jnp.broadcast_to(roots[:, b : b + 1], (tile, LANES))

    rim_zero = jnp.zeros((send_most, tile, LANES), jnp.bfloat16)

    @pl.when(me == 0)
    def _():
        for i in range(pairs):
            exts[i][blocks : blocks + send_most] = rim_zero

    @pl.when(me == n - 1)
    def _():
        for i in range(pairs):
            exts[i][blocks + send_most :] = rim_zero

    def rim_copy(i, side):
        first = blocks if side == 1 else blocks + send_most
        to = me + 1 if side == 1 else me - 1
        return pltpu.make_async_remote_copy(
            src_ref=sends[i].at[side],
            dst_ref=exts[i].at[pl.ds(first, send_most)],
            send_sem=rim_send_sem.at[i, side],
            recv_sem=rim_recv_sem.at[i, side],
            device_id=(to,),
            device_id_type=MESH,
        )

    def send(i):
        source = locals_[i]
        picked = []
        for q in range(hub_dev):
            row = hubs_ref[q]
            near = groups[i][lax.div(row, 16)].astype(jnp.float32)
            here = lax.broadcasted_iota(jnp.int32, near.shape, 0) == lax.rem(row, 16)
            picked.append(jnp.sum(jnp.where(here, near, 0.0), axis=0, keepdims=True))
        packed = jnp.concatenate(picked, axis=0).astype(jnp.bfloat16)
        hub_sends[i][...] = packed
        hub_bufs[i][me] = packed

        def spread(step, carry):
            pltpu.make_async_remote_copy(
                src_ref=hub_sends[i],
                dst_ref=hub_bufs[i].at[me],
                send_sem=hub_send_sem.at[i],
                recv_sem=hub_recv_sem.at[i],
                device_id=(lax.rem(me + step, n),),
                device_id_type=MESH,
            ).start()
            return carry

        lax.fori_loop(1, n, spread, 0)
        for side in range(2):
            for s in range(send_most):
                block = source[listed_ref[0, side, s]]
                keep = jnp.where(s < count_ref[0, side], 1.0, 0.0).astype(jnp.float32)
                sends[i][side, s] = (block.astype(jnp.float32) * keep).astype(jnp.bfloat16)

        @pl.when(me < n - 1)
        def _():
            rim_copy(i, 1).start()

        @pl.when(me > 0)
        def _():
            rim_copy(i, 0).start()

    def prepare(c):
        def one(b, carry):
            rows = pl.ds(pl.multiple_of(b * tile, tile), tile)
            if c < f_chunks:
                x = features[rows, c * LANES : (c + 1) * LANES]
            else:
                x = embeddings[rows, (c - f_chunks) * LANES : (c - f_chunks + 1) * LANES]
            z = (x.astype(jnp.float32) * inv[b]).astype(jnp.bfloat16)
            locals_[c][b] = z
            groups[c][pl.ds(b * per, per)] = z.reshape(per, 16, LANES)
            exts[c][b] = z
            return carry

        lax.fori_loop(0, blocks, one, 0)

    prepare(0)
    pl.semaphore_wait(barrier, n - 1)
    send(0)
    for c in range(1, chunks):
        prepare(c)
        send(c)

    def drain(i, sem):
        some = hub_bufs[i].at[pl.ds(0, n - 1)]
        pltpu.make_async_copy(some, some, sem.at[i]).wait()

    for hop in range(HOPS):
        for c in range(chunks):
            i = hop * chunks + c
            j = i + chunks
            drain(i, hub_recv_sem)

            @pl.when(me > 0)
            def _():
                rim_copy(i, 1).wait_recv()

            @pl.when(me < n - 1)
            def _():
                rim_copy(i, 0).wait_recv()

            hubs = hub_bufs[i][...].reshape(n * hub_dev, LANES)

            def one(b, carry):
                rows = pl.ds(pl.multiple_of(b * tile, tile), tile)
                left = jnp.concatenate([tiles[b, k] for k in range(taps)], axis=1)
                right = jnp.concatenate(
                    [exts[i][cols_ref[b, k]] for k in range(taps)], axis=0
                )
                y = jnp.dot(left, right, preferred_element_type=jnp.float32)
                y = y + jnp.dot(weight[rows, :], hubs, preferred_element_type=jnp.float32)
                x = (y * inv[b]).astype(jnp.bfloat16)
                if c < f_chunks:
                    out_f[hop, rows, c * LANES : (c + 1) * LANES] = x
                else:
                    e = c - f_chunks
                    out_e[hop, rows, e * LANES : (e + 1) * LANES] = x
                if hop + 1 < HOPS:
                    z = (x.astype(jnp.float32) * inv[b]).astype(jnp.bfloat16)
                    locals_[j][b] = z
                    groups[j][pl.ds(b * per, per)] = z.reshape(per, 16, LANES)
                    exts[j][b] = z
                return carry

            lax.fori_loop(0, blocks, one, 0)
            if hop + 1 < HOPS:
                send(j)

    for i in range(pairs):
        drain(i, hub_send_sem)

        @pl.when(me < n - 1)
        def _():
            rim_copy(i, 1).wait_send()

        @pl.when(me > 0)
        def _():
            rim_copy(i, 0).wait_send()


def body(
    features, embeddings, tile_values, tile_columns, send_blocks, send_count,
    hub_rows, hub_weight, degree,
):
    n = lax.axis_size("dom")
    rows = features.shape[0]
    blocks, taps, tile, _ = tile_values.shape
    send_most = send_blocks.shape[2]
    hub_dev = hub_rows.shape[0]
    f_chunks = features.shape[1] // LANES
    chunks = f_chunks + embeddings.shape[1] // LANES
    pairs = HOPS * chunks
    sizes = (blocks, tile, taps, send_most, hub_dev, chunks, f_chunks)
    smem = pl.BlockSpec(memory_space=pltpu.SMEM)
    vmem = pl.BlockSpec(memory_space=pltpu.VMEM)
    bf16 = jnp.bfloat16
    return pl.pallas_call(
        functools.partial(kernel, n, sizes),
        out_shape=(
            jax.ShapeDtypeStruct((HOPS, rows, features.shape[1]), bf16),
            jax.ShapeDtypeStruct((HOPS, rows, embeddings.shape[1]), bf16),
        ),
        in_specs=[smem] * 4 + [vmem] * 5,
        out_specs=(vmem, vmem),
        scratch_shapes=[pltpu.VMEM((blocks, tile, LANES), bf16)] * pairs
        + [pltpu.VMEM((rows // 16, 16, LANES), bf16)] * pairs
        + [pltpu.VMEM((blocks + 2 * send_most, tile, LANES), bf16)] * pairs
        + [pltpu.VMEM((2, send_most, tile, LANES), bf16)] * pairs
        + [pltpu.VMEM((hub_dev, LANES), bf16)] * pairs
        + [pltpu.VMEM((n, hub_dev, LANES), bf16)] * pairs
        + [
            pltpu.VMEM((blocks, tile, LANES), jnp.float32),
            pltpu.SemaphoreType.DMA((pairs, 2)),
            pltpu.SemaphoreType.DMA((pairs, 2)),
            pltpu.SemaphoreType.DMA((pairs,)),
            pltpu.SemaphoreType.DMA((pairs,)),
        ],
        compiler_params=pltpu.CompilerParams(collective_id=0, has_side_effects=True),
    )(
        tile_columns, send_blocks, send_count, hub_rows,
        features, embeddings, tile_values, hub_weight,
        degree.reshape(blocks, tile),
    )


def solution(mesh):
    placed = (
        P("dom", None),
        P("dom", None),
        P("dom", None, None, None),
        P("dom", None),
        P("dom", None, None),
        P("dom", None),
        P("dom"),
        P("dom", None),
        P("dom"),
    )
    return jax.shard_map(
        body,
        mesh=mesh,
        in_specs=placed,
        out_specs=(P(None, "dom", None), P(None, "dom", None)),
        check_vma=False,
    )
```

time: 220 us -> 51.6 us (0.23)
  blocking collectives: 116 us -> 0 us
  Pallas kernels: 0 us -> 42.8 us
  local copies, waits for them, and re-layouts: 47.2 us -> 7.8 us
  matrix products: 24.9 us -> 0 us
  starting transfers between devices: 17.5 us -> 0 us
  other arithmetic: 11.9 us -> 0 us
    all_gather x3 -> x0, blocking collectives: 116 us -> none  [body(): gathered_hubs = lax.all_gather(hub_local, 'dom', axis=0, tiled=True)]
    pallas_call x0 -> x1, Pallas kernels: none -> 42.8 us  [body(): pl.pallas_call(functools.partial(kernel, n, sizes), out_shape=(jax.ShapeD...]
    dot_general x6 -> x0, matrix products: 24.9 us -> none  [the longest x3 14.9 us: body(): jnp.einsum('bkij,bkjw->biw', tile_values, picked, preferred_element_type=...]
    gather x9 -> x0, local copies, waits for them, and re-layouts: 18 us -> none  [the longest x3 10.5 us: body(): picked = extended[tile_columns]]
    ppermute x6 -> x0, starting transfers between devices: 17.5 us -> none  [shifted(): lax.ppermute(value, axis, [(source, source + steps) for source in range(i...]
    reshape x5 -> x0, local copies, waits for them, and re-layouts: 13.2 us -> none  [the longest x3 9.84 us: body(): summed = local_part.reshape(row_count, feature_width) + hub_sum]
    concatenate x3 -> x0, other arithmetic: 5.18 us -> none  [body(): jnp.concatenate([blocked, from_left.reshape(send_most, tile_size, feature...]
    convert_element_type x2 -> x0, other arithmetic: 3.24 us -> none  [body(): scaled = (current.astype(jnp.float32) * inverse_root).astype(jnp.bfloat16)]
  transfers between devices with their start and end apart: 6 -> 0, of which waited for: 0 -> 0; matrix products, arithmetic and copies ran while one was open for 6% -> 0% of each run, Pallas kernels for 0% -> 0%
where the time goes in v1:
time: 51.6 us; the launch traced here: 51.3 us
  Pallas kernels  42.8 us (83%)
  local copies, waits for them, and re-layouts  7.8 us (15%)
  between operations  0.65 us (1%)
    pallas_call x1, Pallas kernels, body(): pl.pallas_call(functools.partial(kernel, n, sizes), out_shape=(jax.ShapeD...  42.8 us
    unnamed x6, local copies, waits for them, and re-layouts  7.8 us

profile of v1, /device:TPU:1, one launch (start us, length us, event | category | flops | bytes accessed | tf_op | source)
XLA Modules:
  0.0 51.3 jit_solution(8751787400628675978)
XLA Ops:
  0.6 1.3 %copy.11.cols_ref = s32[8,4]{1,0:T(8,128)} copy(s32[8,4]{0,1:T(4,128)} %param.12) | data formatting | bytes 256 | tf_op args[3]
  2.0 1.7 %copy.12.weight = bf16[1024,64]{1,0:T(8,128)(2,1)} copy(bf16[1024,64]{0,1:T(8,128)(2,1)} %param.16) | data formatting | bytes 262144 | tf_op args[7]
  3.7 42.8 %shard_map.104 = (bf16[3,1024,512]{2,1,0:T(8,128)(2,1)}, bf16[3,1024,128]{2,1,0:T(8,128)(2,1)}) custom-call(s32[8,4]{1,0:T(8,128)} %copy.11.cols_ref, s32[1,2,2]{2,1,0:T(2,128)} %listed_ref.1, s32[1,2]{1,0:T(1,128)} %count_ref.1, s32[2]{0:T(128)} %hubs_ref.1, bf16[1024,512]{1,0:T(8,128)(2,1)} %features.1, bf16[1024,128]{1,0:T(8,128)(2,1)} %embeddings.1, ...), custom_call_target="tpu_custom_call" | custom-call | tf_op jit(solution)/shard_map/pallas_call | solution.py:200
  46.6 0.0 copy-start
  46.6 3.8 %copy.15 = bf16[3,1024,512]{2,1,0:T(8,128)(2,1)} copy(bf16[3,1024,512]{2,1,0:T(8,128)(2,1)} %get-tuple-element.4) | data formatting | bytes 6291456
  50.4 0.0 copy-done
  50.4 0.9 %copy.16 = bf16[3,1024,128]{2,1,0:T(8,128)(2,1)} copy(bf16[3,1024,128]{2,1,0:T(8,128)(2,1)S(1)} %copy-done) | data formatting | bytes 1572864
Async XLA Ops:
  46.6 3.8 %copy-start = (bf16[3,1024,128]{2,1,0:T(8,128)(2,1)S(1)}, bf16[3,1024,128]{2,1,0:T(8,128)(2,1)}, u32[]{:S(2)}) copy-start(bf16[3,1024,128]{2,1,0:T(8,128)(2,1)} %get-tuple-element.5) | copy-start | bytes 2359300

commit v2 on v1

--- a/solution.py
+++ b/solution.py
@@ -9,12 +9,13 @@
 
 HOPS = 3
 LANES = 128
+VMEM = 67043328
 MESH = pl.DeviceIdType.MESH
 
 
 def kernel(
     n, sizes, cols_ref, listed_ref, count_ref, hubs_ref,
-    features, embeddings, tiles, weight, degree,
+    features_hbm, embeddings_hbm, tiles_hbm, weight_hbm, degree_hbm,
     out_f, out_e, *scratch,
 ):
     blocks, tile, taps, send_most, hub_dev, chunks, f_chunks = sizes
@@ -23,8 +24,23 @@
     scratch = list(scratch)
     take = lambda count: [scratch.pop(0) for _ in range(count)]
     locals_, groups, exts, sends, hub_sends, hub_bufs = (take(pairs) for _ in range(6))
-    inv, rim_send_sem, rim_recv_sem, hub_send_sem, hub_recv_sem = scratch
+    features, embeddings, tiles, weight_t, degree, weight, inv, load_sem, rim_send_sem, rim_recv_sem, hub_send_sem, hub_recv_sem = scratch
     me = lax.axis_index("dom")
+
+    loads = [
+        pltpu.make_async_copy(source, held, load_sem.at[q])
+        for q, (source, held) in enumerate(
+            (
+                (degree_hbm, degree),
+                (features_hbm, features),
+                (embeddings_hbm, embeddings),
+                (tiles_hbm, tiles),
+                (weight_hbm, weight_t),
+            )
+        )
+    ]
+    for load in loads:
+        load.start()
 
     barrier = pltpu.get_barrier_semaphore()
 
@@ -36,6 +52,7 @@
 
     lax.fori_loop(1, n, greet, 0)
 
+    loads[0].wait()
     roots = lax.rsqrt(degree[...].astype(jnp.float32)).T
     for b in range(blocks):
         inv[b] = jnp.broadcast_to(roots[:, b : b + 1], (tile, LANES))
@@ -117,6 +134,8 @@
 
         lax.fori_loop(0, blocks, one, 0)
 
+    loads[1].wait()
+    loads[2].wait()
     prepare(0)
     pl.semaphore_wait(barrier, n - 1)
     send(0)
@@ -124,6 +143,10 @@
         prepare(c)
         send(c)
 
+    loads[3].wait()
+    loads[4].wait()
+    weight[...] = weight_t[...].T
+
     def drain(i, sem):
         some = hub_bufs[i].at[pl.ds(0, n - 1)]
         pltpu.make_async_copy(some, some, sem.at[i]).wait()
@@ -148,7 +171,7 @@
                 rows = pl.ds(pl.multiple_of(b * tile, tile), tile)
                 left = jnp.concatenate([tiles[b, k] for k in range(taps)], axis=1)
                 right = jnp.concatenate(
-                    [exts[i][cols_ref[b, k]] for k in range(taps)], axis=0
+                    [exts[i][cols_ref[k, b]] for k in range(taps)], axis=0
                 )
                 y = jnp.dot(left, right, preferred_element_type=jnp.float32)
                 y = y + jnp.dot(weight[rows, :], hubs, preferred_element_type=jnp.float32)
@@ -194,16 +217,17 @@
     chunks = f_chunks + embeddings.shape[1] // LANES
     pairs = HOPS * chunks
     sizes = (blocks, tile, taps, send_most, hub_dev, chunks, f_chunks)
+    out_bytes = HOPS * rows * chunks * LANES * 2
     smem = pl.BlockSpec(memory_space=pltpu.SMEM)
     vmem = pl.BlockSpec(memory_space=pltpu.VMEM)
     bf16 = jnp.bfloat16
     return pl.pallas_call(
         functools.partial(kernel, n, sizes),
         out_shape=(
-            jax.ShapeDtypeStruct((HOPS, rows, features.shape[1]), bf16),
-            jax.ShapeDtypeStruct((HOPS, rows, embeddings.shape[1]), bf16),
+            pltpu.VMEM((HOPS, rows, features.shape[1]), bf16),
+            pltpu.VMEM((HOPS, rows, embeddings.shape[1]), bf16),
         ),
-        in_specs=[smem] * 4 + [vmem] * 5,
+        in_specs=[smem] * 4 + [pl.BlockSpec(memory_space=pltpu.HBM)] * 5,
         out_specs=(vmem, vmem),
         scratch_shapes=[pltpu.VMEM((blocks, tile, LANES), bf16)] * pairs
         + [pltpu.VMEM((rows // 16, 16, LANES), bf16)] * pairs
@@ -212,16 +236,25 @@
         + [pltpu.VMEM((hub_dev, LANES), bf16)] * pairs
         + [pltpu.VMEM((n, hub_dev, LANES), bf16)] * pairs
         + [
+            pltpu.VMEM(features.shape, bf16),
+            pltpu.VMEM(embeddings.shape, bf16),
+            pltpu.VMEM(tile_values.shape, bf16),
+            pltpu.VMEM((n * hub_dev, rows), bf16),
+            pltpu.VMEM((blocks, tile), jnp.int32),
+            pltpu.VMEM((rows, n * hub_dev), bf16),
             pltpu.VMEM((blocks, tile, LANES), jnp.float32),
+            pltpu.SemaphoreType.DMA((5,)),
             pltpu.SemaphoreType.DMA((pairs, 2)),
             pltpu.SemaphoreType.DMA((pairs, 2)),
             pltpu.SemaphoreType.DMA((pairs,)),
             pltpu.SemaphoreType.DMA((pairs,)),
         ],
-        compiler_params=pltpu.CompilerParams(collective_id=0, has_side_effects=True),
+        compiler_params=pltpu.CompilerParams(
+            collective_id=0, has_side_effects=True, vmem_limit_bytes=VMEM - out_bytes
+        ),
     )(
-        tile_columns, send_blocks, send_count, hub_rows,
-        features, embeddings, tile_values, hub_weight,
+        tile_columns.T, send_blocks, send_count, hub_rows,
+        features, embeddings, tile_values, hub_weight.T,
         degree.reshape(blocks, tile),
     )
 

time: 51.6 us -> 43.6 us (0.84)
  local copies, waits for them, and re-layouts: 7.8 us -> 2.55 us
  Pallas kernels: 42.8 us -> 40.1 us
    unnamed x6 -> x2, local copies, waits for them, and re-layouts: 7.8 us -> 2.55 us
    pallas_call x1, Pallas kernels: 42.8 us -> 40.1 us  [body(): pl.pallas_call(functools.partial(kernel, n, sizes), out_shape=(pltpu.VMEM...]
where the time goes in v2:
time: 43.6 us; the launch traced here: 43.3 us
  Pallas kernels  40.1 us (92%)
  local copies, waits for them, and re-layouts  2.55 us (6%)
  between operations  0.64 us (1%)
    pallas_call x1, Pallas kernels, body(): pl.pallas_call(functools.partial(kernel, n, sizes), out_shape=(pltpu.VMEM...  40.1 us
    unnamed x2, local copies, waits for them, and re-layouts  2.55 us

profile of v2, /device:TPU:1, one launch (start us, length us, event | category | flops | bytes accessed | tf_op | source)
XLA Modules:
  0.0 43.3 jit_solution(15157787518348710783)
XLA Ops:
  0.6 40.1 %shard_map.104 = (bf16[3,1024,512]{2,1,0:T(8,128)(2,1)S(1)}, bf16[3,1024,128]{2,1,0:T(8,128)(2,1)S(1)}) custom-call(s32[4,8]{1,0:T(4,128)} %bitcast.5, s32[1,2,2]{2,1,0:T(2,128)} %listed_ref.1, s32[1,2]{1,0:T(1,128)} %count_ref.1, s32[2]{0:T(128)} %hubs_ref.1, bf16[1024,512]{1,0:T(8,128)(2,1)} %features_hbm.1, bf16[1024,128]{1,0:T(8,128)(2,1)} %embeddings_hbm.1, ...), custom_call_target="tpu_custom_call" | custom-call | tf_op jit(solution)/shard_map/pallas_call | solution.py:224
  40.7 1.7 %copy.13 = bf16[3,1024,512]{2,1,0:T(8,128)(2,1)} copy(bf16[3,1024,512]{2,1,0:T(8,128)(2,1)S(1)} %get-tuple-element.2) | data formatting | bytes 6291456
  42.4 0.9 %copy.14 = bf16[3,1024,128]{2,1,0:T(8,128)(2,1)} copy(bf16[3,1024,128]{2,1,0:T(8,128)(2,1)S(1)} %get-tuple-element.3) | data formatting | bytes 1572864

commit v3 on v2

--- a/solution.py
+++ b/solution.py
@@ -9,8 +9,14 @@
 
 HOPS = 3
 LANES = 128
+WIDTH = 256
+UNROLL = 4
 VMEM = 67043328
 MESH = pl.DeviceIdType.MESH
+
+
+def cut(which, columns):
+    return [(which, at, min(WIDTH, columns - at)) for at in range(0, columns, WIDTH)]
 
 
 def kernel(
@@ -18,7 +24,8 @@
     features_hbm, embeddings_hbm, tiles_hbm, weight_hbm, degree_hbm,
     out_f, out_e, *scratch,
 ):
-    blocks, tile, taps, send_most, hub_dev, chunks, f_chunks = sizes
+    blocks, tile, taps, send_most, hub_dev, pieces = sizes
+    chunks = len(pieces)
     per = tile // 16
     pairs = HOPS * chunks
     scratch = list(scratch)
@@ -57,17 +64,18 @@
     for b in range(blocks):
         inv[b] = jnp.broadcast_to(roots[:, b : b + 1], (tile, LANES))
 
-    rim_zero = jnp.zeros((send_most, tile, LANES), jnp.bfloat16)
+    def wide(b, width):
+        return jnp.concatenate([inv[b]] * (width // LANES), axis=1)
 
     @pl.when(me == 0)
     def _():
         for i in range(pairs):
-            exts[i][blocks : blocks + send_most] = rim_zero
+            exts[i][blocks : blocks + send_most] = jnp.zeros((send_most,) + exts[i].shape[1:], jnp.bfloat16)
 
     @pl.when(me == n - 1)
     def _():
         for i in range(pairs):
-            exts[i][blocks + send_most :] = rim_zero
+            exts[i][blocks + send_most :] = jnp.zeros((send_most,) + exts[i].shape[1:], jnp.bfloat16)
 
     def rim_copy(i, side):
         first = blocks if side == 1 else blocks + send_most
@@ -120,19 +128,18 @@
             rim_copy(i, 0).start()
 
     def prepare(c):
+        which, at, width = pieces[c]
+
         def one(b, carry):
             rows = pl.ds(pl.multiple_of(b * tile, tile), tile)
-            if c < f_chunks:
-                x = features[rows, c * LANES : (c + 1) * LANES]
-            else:
-                x = embeddings[rows, (c - f_chunks) * LANES : (c - f_chunks + 1) * LANES]
-            z = (x.astype(jnp.float32) * inv[b]).astype(jnp.bfloat16)
+            x = (features, embeddings)[which][rows, at : at + width]
+            z = (x.astype(jnp.float32) * wide(b, width)).astype(jnp.bfloat16)
             locals_[c][b] = z
-            groups[c][pl.ds(b * per, per)] = z.reshape(per, 16, LANES)
+            groups[c][pl.ds(b * per, per)] = z.reshape(per, 16, width)
             exts[c][b] = z
             return carry
 
-        lax.fori_loop(0, blocks, one, 0)
+        lax.fori_loop(0, blocks, one, 0, unroll=UNROLL)
 
     loads[1].wait()
     loads[2].wait()
@@ -155,6 +162,7 @@
         for c in range(chunks):
             i = hop * chunks + c
             j = i + chunks
+            which, at, width = pieces[c]
             drain(i, hub_recv_sem)
 
             @pl.when(me > 0)
@@ -165,7 +173,7 @@
             def _():
                 rim_copy(i, 0).wait_recv()
 
-            hubs = hub_bufs[i][...].reshape(n * hub_dev, LANES)
+            hubs = hub_bufs[i][...].reshape(n * hub_dev, width)
 
             def one(b, carry):
                 rows = pl.ds(pl.multiple_of(b * tile, tile), tile)
@@ -175,20 +183,17 @@
                 )
                 y = jnp.dot(left, right, preferred_element_type=jnp.float32)
                 y = y + jnp.dot(weight[rows, :], hubs, preferred_element_type=jnp.float32)
-                x = (y * inv[b]).astype(jnp.bfloat16)
-                if c < f_chunks:
-                    out_f[hop, rows, c * LANES : (c + 1) * LANES] = x
-                else:
-                    e = c - f_chunks
-                    out_e[hop, rows, e * LANES : (e + 1) * LANES] = x
+                root = wide(b, width)
+                x = (y * root).astype(jnp.bfloat16)
+                (out_f, out_e)[which][hop, rows, at : at + width] = x
                 if hop + 1 < HOPS:
-                    z = (x.astype(jnp.float32) * inv[b]).astype(jnp.bfloat16)
+                    z = (x.astype(jnp.float32) * root).astype(jnp.bfloat16)
                     locals_[j][b] = z
-                    groups[j][pl.ds(b * per, per)] = z.reshape(per, 16, LANES)
+                    groups[j][pl.ds(b * per, per)] = z.reshape(per, 16, width)
                     exts[j][b] = z
                 return carry
 
-            lax.fori_loop(0, blocks, one, 0)
+            lax.fori_loop(0, blocks, one, 0, unroll=UNROLL)
             if hop + 1 < HOPS:
                 send(j)
 
@@ -213,11 +218,10 @@
     blocks, taps, tile, _ = tile_values.shape
     send_most = send_blocks.shape[2]
     hub_dev = hub_rows.shape[0]
-    f_chunks = features.shape[1] // LANES
-    chunks = f_chunks + embeddings.shape[1] // LANES
-    pairs = HOPS * chunks
-    sizes = (blocks, tile, taps, send_most, hub_dev, chunks, f_chunks)
-    out_bytes = HOPS * rows * chunks * LANES * 2
+    pieces = cut(0, features.shape[1]) + cut(1, embeddings.shape[1])
+    sizes = (blocks, tile, taps, send_most, hub_dev, pieces)
+    widths = [width for _, _, width in pieces] * HOPS
+    out_bytes = HOPS * rows * (features.shape[1] + embeddings.shape[1]) * 2
     smem = pl.BlockSpec(memory_space=pltpu.SMEM)
     vmem = pl.BlockSpec(memory_space=pltpu.VMEM)
     bf16 = jnp.bfloat16
@@ -229,12 +233,18 @@
         ),
         in_specs=[smem] * 4 + [pl.BlockSpec(memory_space=pltpu.HBM)] * 5,
         out_specs=(vmem, vmem),
-        scratch_shapes=[pltpu.VMEM((blocks, tile, LANES), bf16)] * pairs
-        + [pltpu.VMEM((rows // 16, 16, LANES), bf16)] * pairs
-        + [pltpu.VMEM((blocks + 2 * send_most, tile, LANES), bf16)] * pairs
-        + [pltpu.VMEM((2, send_most, tile, LANES), bf16)] * pairs
-        + [pltpu.VMEM((hub_dev, LANES), bf16)] * pairs
-        + [pltpu.VMEM((n, hub_dev, LANES), bf16)] * pairs
+        scratch_shapes=[
+            pltpu.VMEM(shape + (width,), bf16)
+            for shape in (
+                (blocks, tile),
+                (rows // 16, 16),
+                (blocks + 2 * send_most, tile),
+                (2, send_most, tile),
+                (hub_dev,),
+                (n, hub_dev),
+            )
+            for width in widths
+        ]
         + [
             pltpu.VMEM(features.shape, bf16),
             pltpu.VMEM(embeddings.shape, bf16),
@@ -244,10 +254,10 @@
             pltpu.VMEM((rows, n * hub_dev), bf16),
             pltpu.VMEM((blocks, tile, LANES), jnp.float32),
             pltpu.SemaphoreType.DMA((5,)),
-            pltpu.SemaphoreType.DMA((pairs, 2)),
-            pltpu.SemaphoreType.DMA((pairs, 2)),
-            pltpu.SemaphoreType.DMA((pairs,)),
-            pltpu.SemaphoreType.DMA((pairs,)),
+            pltpu.SemaphoreType.DMA((len(widths), 2)),
+            pltpu.SemaphoreType.DMA((len(widths), 2)),
+            pltpu.SemaphoreType.DMA((len(widths),)),
+            pltpu.SemaphoreType.DMA((len(widths),)),
         ],
         compiler_params=pltpu.CompilerParams(
             collective_id=0, has_side_effects=True, vmem_limit_bytes=VMEM - out_bytes

time: 43.6 us -> 37.5 us (0.86)
  Pallas kernels: 40.1 us -> 34.1 us
    pallas_call x1, Pallas kernels: 40.1 us -> 34.1 us  [body(): pl.pallas_call(functools.partial(kernel, n, sizes), out_shape=(pltpu.VMEM...]
where the time goes in v3:
time: 37.5 us; the launch traced here: 37.3 us
  Pallas kernels  34.1 us (91%)
  local copies, waits for them, and re-layouts  2.55 us (7%)
  between operations  0.64 us (2%)
    pallas_call x1, Pallas kernels, body(): pl.pallas_call(functools.partial(kernel, n, sizes), out_shape=(pltpu.VMEM...  34.1 us
    unnamed x2, local copies, waits for them, and re-layouts  2.55 us

profile of v3, /device:TPU:1, one launch (start us, length us, event | category | flops | bytes accessed | tf_op | source)
XLA Modules:
  0.0 37.3 jit_solution(962404384343248926)
XLA Ops:
  0.6 34.1 %shard_map.104 = (bf16[3,1024,512]{2,1,0:T(8,128)(2,1)S(1)}, bf16[3,1024,128]{2,1,0:T(8,128)(2,1)S(1)}) custom-call(s32[4,8]{1,0:T(4,128)} %bitcast.5, s32[1,2,2]{2,1,0:T(2,128)} %listed_ref.1, s32[1,2]{1,0:T(1,128)} %count_ref.1, s32[2]{0:T(128)} %hubs_ref.1, bf16[1024,512]{1,0:T(8,128)(2,1)} %features_hbm.1, bf16[1024,128]{1,0:T(8,128)(2,1)} %embeddings_hbm.1, ...), custom_call_target="tpu_custom_call" | custom-call | tf_op jit(solution)/shard_map/pallas_call | solution.py:228
  34.8 1.7 %copy.13 = bf16[3,1024,512]{2,1,0:T(8,128)(2,1)} copy(bf16[3,1024,512]{2,1,0:T(8,128)(2,1)S(1)} %get-tuple-element.2) | data formatting | bytes 6291456
  36.4 0.9 %copy.14 = bf16[3,1024,128]{2,1,0:T(8,128)(2,1)} copy(bf16[3,1024,128]{2,1,0:T(8,128)(2,1)S(1)} %get-tuple-element.3) | data formatting | bytes 1572864

commit v4 on v3

--- a/solution.py
+++ b/solution.py
@@ -89,7 +89,7 @@
             device_id_type=MESH,
         )
 
-    def send(i):
+    def stage(i):
         source = locals_[i]
         picked = []
         for q in range(hub_dev):
@@ -101,6 +101,14 @@
         hub_sends[i][...] = packed
         hub_bufs[i][me] = packed
 
+        for side in range(2):
+            for s in range(send_most):
+                block = source[listed_ref[0, side, s]]
+                keep = jnp.where(s < count_ref[0, side], 1.0, 0.0).astype(jnp.float32)
+                sends[i][side, s] = (block.astype(jnp.float32) * keep).astype(jnp.bfloat16)
+
+
+    def launch(i):
         def spread(step, carry):
             pltpu.make_async_remote_copy(
                 src_ref=hub_sends[i],
@@ -113,11 +121,6 @@
             return carry
 
         lax.fori_loop(1, n, spread, 0)
-        for side in range(2):
-            for s in range(send_most):
-                block = source[listed_ref[0, side, s]]
-                keep = jnp.where(s < count_ref[0, side], 1.0, 0.0).astype(jnp.float32)
-                sends[i][side, s] = (block.astype(jnp.float32) * keep).astype(jnp.bfloat16)
 
         @pl.when(me < n - 1)
         def _():
@@ -143,12 +146,12 @@
 
     loads[1].wait()
     loads[2].wait()
-    prepare(0)
+    for c in range(chunks):
+        prepare(c)
+        stage(c)
     pl.semaphore_wait(barrier, n - 1)
-    send(0)
-    for c in range(1, chunks):
-        prepare(c)
-        send(c)
+    for c in range(chunks):
+        launch(c)
 
     loads[3].wait()
     loads[4].wait()
@@ -195,7 +198,8 @@
 
             lax.fori_loop(0, blocks, one, 0, unroll=UNROLL)
             if hop + 1 < HOPS:
-                send(j)
+                stage(j)
+                launch(j)
 
     for i in range(pairs):
         drain(i, hub_send_sem)
@@ -207,6 +211,17 @@
         @pl.when(me > 0)
         def _():
             rim_copy(i, 0).wait_send()
+
+
+def flush(held_f, held_e, out_f, out_e, sem):
+    copies = [
+        pltpu.make_async_copy(held_f, out_f, sem.at[0]),
+        pltpu.make_async_copy(held_e, out_e, sem.at[1]),
+    ]
+    for copy in copies:
+        copy.start()
+    for copy in copies:
+        copy.wait()
 
 
 def body(
@@ -225,7 +240,7 @@
     smem = pl.BlockSpec(memory_space=pltpu.SMEM)
     vmem = pl.BlockSpec(memory_space=pltpu.VMEM)
     bf16 = jnp.bfloat16
-    return pl.pallas_call(
+    held = pl.pallas_call(
         functools.partial(kernel, n, sizes),
         out_shape=(
             pltpu.VMEM((HOPS, rows, features.shape[1]), bf16),
@@ -267,6 +282,15 @@
         features, embeddings, tile_values, hub_weight.T,
         degree.reshape(blocks, tile),
     )
+    hbm = pl.BlockSpec(memory_space=pltpu.HBM)
+    return pl.pallas_call(
+        flush,
+        out_shape=tuple(jax.ShapeDtypeStruct(h.shape, h.dtype) for h in held),
+        in_specs=[vmem] * 2,
+        out_specs=(hbm, hbm),
+        scratch_shapes=[pltpu.SemaphoreType.DMA((2,))],
+        compiler_params=pltpu.CompilerParams(vmem_limit_bytes=2**20),
+    )(*held)
 
 
 def solution(mesh):

time: 37.5 us -> 36.7 us (0.979)
  local copies, waits for them, and re-layouts: 2.55 us -> 0 us
  Pallas kernels: 34.1 us -> 35.9 us
    unnamed x2 -> x0, local copies, waits for them, and re-layouts: 2.55 us -> none
    pallas_call x0 -> x1, Pallas kernels: none -> 1.93 us  [body(): pl.pallas_call(flush, out_shape=tuple((jax.ShapeDtypeStruct(h.shape, h.dt...]
where the time goes in v4:
time: 36.7 us; the launch traced here: 36.5 us
  Pallas kernels  35.9 us (98%)
  between operations  0.64 us (2%)
    pallas_call x1, Pallas kernels, body(): pl.pallas_call(functools.partial(kernel, n, sizes), out_shape=(pltpu.VMEM...  33.9 us
    pallas_call x1, Pallas kernels, body(): pl.pallas_call(flush, out_shape=tuple((jax.ShapeDtypeStruct(h.shape, h.dt...  1.93 us

profile of v4, /device:TPU:1, one launch (start us, length us, event | category | flops | bytes accessed | tf_op | source)
XLA Modules:
  0.0 36.5 jit_solution(827830104275543946)
XLA Ops:
  0.6 33.9 %shard_map.104 = (bf16[3,1024,512]{2,1,0:T(8,128)(2,1)S(1)}, bf16[3,1024,128]{2,1,0:T(8,128)(2,1)S(1)}) custom-call(s32[4,8]{1,0:T(4,128)} %bitcast.5, s32[1,2,2]{2,1,0:T(2,128)} %listed_ref.1, s32[1,2]{1,0:T(1,128)} %count_ref.1, s32[2]{0:T(128)} %hubs_ref.1, bf16[1024,512]{1,0:T(8,128)(2,1)} %features_hbm.1, bf16[1024,128]{1,0:T(8,128)(2,1)} %embeddings_hbm.1, ...), custom_call_target="tpu_custom_call" | custom-call | tf_op jit(solution)/shard_map/pallas_call | solution.py:243
  34.6 1.9 %shard_map.105 = (bf16[3,1024,512]{2,1,0:T(8,128)(2,1)}, bf16[3,1024,128]{2,1,0:T(8,128)(2,1)}) custom-call(bf16[3,1024,512]{2,1,0:T(8,128)(2,1)S(1)} %get-tuple-element.4.held_f, bf16[3,1024,128]{2,1,0:T(8,128)(2,1)S(1)} %get-tuple-element.5.held_e), custom_call_target="tpu_custom_call" | custom-call | tf_op jit(solution)/shard_map/pallas_call | solution.py:286
